TPU v7x, 32 devices: a whole 2x2x4 slice. The times are simulated.
32 devices in a mesh: parts: 2 (over y), mem: 4 (over z), space: 4 (over x, core).
Axes of the slice: x: 2, y: 2, z: 4, core: 2. Of those that a mesh axis runs over, the one named last changes fastest.
Arguments:
- ensemble: bfloat16 [64, 70, 8192], P('mem', None, ('parts', 'space')), parts along dimension 2, may hold values from -6 to 6
- transform: bfloat16 [128, 64], P('parts'), parts along dimension 0, may hold values from -0.75 to 0.75
- obs_operator: bfloat16 [16, 70], replicated, may hold values from -0.75 to 0.75
- obs_weight: float32 [16, 8192], P(None, ('parts', 'space')), parts along dimension 1, may hold values from 0.25 to 40, as said below
Outputs:
- analysis: bfloat16 [64, 70, 8192], P('mem', None, ('parts', 'space')), parts along dimension 2
- prior_gram: float32 [128, 64], P('parts'), parts along dimension 0
- posterior_gram: float32 [128, 64], P('parts'), parts along dimension 0
There are 2 independent parts, one for each index of `parts`. A program takes and returns all parts, laid end to end along the dimension named above; an argument that names none is the same for every part. Nothing has to cross between parts.
Inputs may be any that keep to these rules, and one draw needn't show every extreme that they name: `obs_weight`: positive.
All inputs are finite; a program needn't handle non-finite values.
Results may differ from a plain program's by a relative error of at most 0.001.
Values may be sent and summed in bfloat16 or wider, within the bound.
A program may use at most 64 MiB of HBM per device.

v0:
```python
import jax
import jax.numpy as jnp
from jax import lax
from jax.sharding import PartitionSpec as P

MEMBERS = 64
HIGHEST = lax.Precision.HIGHEST


def gram_terms(observed, weights):
    departures = observed - jnp.sum(observed, axis=0) / MEMBERS
    weighted = departures * weights[None, :, :]
    partial_gram = jnp.einsum("ioc,joc->ij", weighted, departures, precision=HIGHEST)
    return (partial_gram, jnp.sum(weights))


def per_device(ensemble, transform, obs_operator, obs_weight):
    local_members = ensemble.shape[0]
    mixing = transform.astype(jnp.float32)
    own_start = lax.axis_index("mem") * local_members
    own_columns = lax.dynamic_slice_in_dim(transform, own_start, local_members, 1)
    keep_mean = 1.0 - jnp.sum(own_columns.astype(jnp.float32), axis=0)
    members_block = lax.all_gather(ensemble, "mem", axis=0, tiled=True)
    combined = jnp.einsum(
        "kj,kvc->jvc", own_columns, members_block, preferred_element_type=jnp.float32
    )
    totals = jnp.sum(members_block, axis=0, dtype=jnp.float32)
    results = (totals, combined)
    totals = results[0]
    combined = results[1]
    member_mean = totals / MEMBERS
    analysis = (combined + member_mean[None, :, :] * keep_mean[:, None, None]).astype(jnp.bfloat16)
    observed = jnp.einsum("ov,mvc->moc", obs_operator, ensemble, preferred_element_type=jnp.float32)
    by_columns = lax.all_to_all(
        observed.astype(jnp.bfloat16), "mem", split_axis=2, concat_axis=0, tiled=True
    ).astype(observed.dtype)
    cells_here = by_columns.shape[2]
    own_weights = lax.dynamic_slice_in_dim(
        obs_weight, lax.axis_index("mem") * cells_here, cells_here, 1
    )
    partial_gram, weight_sum = gram_terms(by_columns, own_weights)
    gram_sum, weight_total = lax.psum((partial_gram, weight_sum), ("mem", "space"))
    prior_gram = gram_sum / weight_total
    carried = jnp.dot(mixing.T, prior_gram, precision=HIGHEST)
    posterior_gram = jnp.dot(carried, mixing, precision=HIGHEST)
    return (analysis, prior_gram, posterior_gram)


def solution(mesh):
    return jax.shard_map(
        per_device,
        mesh=mesh,
        in_specs=(
            P("mem", None, ("parts", "space")),
            P("parts", None),
            P(),
            P(None, ("parts", "space")),
        ),
        out_specs=(P("mem", None, ("parts", "space")), P("parts", None), P("parts", None)),
        check_vma=False,
    )
```

profile of v0, /device:TPU:0, one launch (start us, length us, event | category | flops | bytes accessed | tf_op | source)
XLA Modules:
  0.0 202.9 jit_solution(353153275937876548)
XLA Ops:
  7.2 0.0 copy-start
  7.2 0.0 all-gather.2.cloned.1.call-start
  7.2 0.7 all-gather.2.cloned.1.call-update
  7.9 3.0 %fusion.7 = bf16[16,16,1024]{2,1,0:T(8,128)(2,1)S(1)} fusion(bf16[16,70,1024]{2,0,1:T(8,128)(2,1)} %param.4, bf16[16,70]{1,0:T(8,128)(2,1)} %param.6), kind=kOutput, calls=%fused_computation.8 | convolution fusion | flops 36962304 | bytes 2820288 | tf_op jit(solution)/shard_map/ov,mvc->moc/dot_general | solution.py:33
  10.9 4.7 %copy.25 = bf16[16,16,1024]{1,0,2:T(8,128)(2,1)} copy(bf16[16,16,1024]{2,1,0:T(8,128)(2,1)S(1)} %fusion.7) | data formatting | bytes 1048576 | tf_op jit(solution)/shard_map/convert_element_type | solution.py:35
  15.6 6.6 %reshape.27 = bf16[4,2,32768]{2,1,0:T(2,128)(2,1)} reshape(bf16[1024,16,16]{2,1,0:T(8,128)(2,1)} %bitcast.28) | data formatting | bytes 1048576
  22.2 6.4 %all-to-all-start = ((bf16[4,2,32768]{2,1,0:T(2,128)(2,1)}), bf16[4,2,32768]{2,1,0:T(2,128)(2,1)S(1)}, u32[]{:S(2)}, u32[]{:S(2)}) async-start(bf16[4,2,32768]{2,1,0:T(2,128)(2,1)} %reshape.27), calls=%async_computation | async-start | bytes 1048576 | tf_op jit(solution)/shard_map/all_to_all | solution.py:34
  28.6 0.0 copy-done
  28.6 0.1 constant_dynamic-slice_fusion.1
  28.7 0.1 copy.28
  28.8 0.1 convert_reduce_fusion.2
  28.9 1.3 fusion.16
  30.2 25.9 %all-to-all-done = bf16[4,2,32768]{2,1,0:T(2,128)(2,1)S(1)} async-done(((bf16[4,2,32768]{2,1,0:T(2,128)(2,1)}), bf16[4,2,32768]{2,1,0:T(2,128)(2,1)S(1)}, u32[]{:S(2)}, u32[]{:S(2)}) %all-to-all-start) | async-done | bytes 524320 | tf_op jit(solution)/shard_map/all_to_all | solution.py:34
  56.1 4.1 %reshape.28 = bf16[1024,16,16]{2,1,0:T(8,128)(2,1)} reshape(bf16[4,2,32768]{2,1,0:T(2,128)(2,1)S(1)} %all-to-all-done) | data formatting | bytes 1048576
  60.2 6.1 %bitcast_convert_fusion = f32[16,16,1024]{1,0,2:T(8,128)} fusion(bf16[1024,16,16]{2,1,0:T(8,128)(2,1)} %reshape.28), kind=kLoop, calls=%fused_computation.22 | loop fusion | flops 262144 | bytes 1572864 | tf_op jit(solution)/shard_map/convert_element_type | solution.py:36
  66.4 6.6 %copy.26 = f32[4,16,16,256]{3,1,0,2:T(8,128)S(1)} copy(f32[4,16,16,256]{2,1,3,0:T(8,128)} %bitcast.27) | data formatting | bytes 2097152 | tf_op jit(solution)/shard_map/convert_element_type | solution.py:36
  72.9 4.2 %convert_reduce_fusion.1 = f32[16,1024]{0,1:T(8,128)S(1)} fusion(bf16[1024,16,16]{2,1,0:T(8,128)(2,1)} %reshape.28), kind=kLoop, calls=%fused_computation.4 | loop fusion | flops 507904 | bytes 589824 | tf_op jit(solution)/shard_map/reduce_sum | solution.py:11
  77.2 0.1 copy.27
  77.3 0.1 bitcast_subtract_fusion
  77.5 1.0 fusion.10
  78.5 63.8 %all-reduce = (f32[64,64]{1,0:T(8,128)S(1)}, f32[]{:T(128)}) all-reduce(f32[64,64]{1,0:T(8,128)S(1)} %fusion.10, f32[]{:T(128)} %get-tuple-element.5), channel_id=1, replica_groups=mesh['parts'=2,'mem'=4,'space'=4] {'mem','space'}, use_global_device_ids=true, to_apply=%region_4.0 | all-reduce | flops 4097 | bytes 32776 | tf_op jit(solution)/shard_map/psum | solution.py:42
  142.3 0.7 broadcast_divide_fusion
  142.9 0.0 copy-start.2
  142.9 0.2 fusion.17
  143.2 0.8 fusion.18
  144.0 42.6 %all-gather.2.cloned.1.call-done = bf16[64,70,1024]{2,0,1:T(8,128)(2,1)} async-done(((bf16[16,70,1024]{2,0,1:T(8,128)(2,1)}), bf16[64,70,1024]{2,0,1:T(8,128)(2,1)}) %all-gather.2.cloned.1.call-update) | async-done | bytes 9175056 | tf_op jit(solution)/shard_map/all_gather | solution.py:23
  186.6 0.0 copy-start.1
  186.6 6.7 %convert_reduce_fusion = f32[70,1024]{1,0:T(8,128)S(1)} fusion(bf16[64,70,1024]{2,0,1:T(8,128)(2,1)} %all-gather.2.cloned.1.call-done), kind=kLoop, calls=%fused_computation | loop fusion | flops 9103360 | bytes 9461760 | tf_op jit(solution)/shard_map/reduce_sum | solution.py:27
  193.3 0.0 copy-done.2
  193.3 0.0 copy-done.1
  193.3 2.8 %add_convert_fusion = bf16[16,70,1024]{2,0,1:T(8,128)(2,1)} fusion(f32[16]{0:T(128)S(1)} %broadcast_subtract_fusion, f32[70,1024]{1,0:T(8,128)S(1)} %broadcast_multiply_fusion, bf16[64,70,1024]{2,0,1:T(8,128)(2,1)S(1)} %copy-done.1, bf16[64,16]{1,0:T(8,128)(2,1)S(1)} %constant_dynamic-slice_fusion.1), kind=kOutput, calls=%fused_computation.1 | convolution fusion | flops 150241280 | bytes 11757632 | tf_op jit(solution)/shard_map/kj,kvc->jvc/dot_general | solution.py:24
  (4 shorter events, 0.1 us)
Async XLA Ops:
  7.2 21.4 %copy-start = (bf16[64,64]{1,0:T(8,128)(2,1)S(1)}, bf16[64,64]{1,0:T(8,128)(2,1)}, u32[]{:S(2)}) copy-start(bf16[64,64]{1,0:T(8,128)(2,1)} %param.5) | copy-start | bytes 24580
  7.2 179.4 %all-gather.2.cloned.1.call-start = ((), (), s32[]{:S(2)}) async-start(), calls=%async_computation.1 | async-start | bytes 11468800 | tf_op jit(solution)/shard_map/all_gather | solution.py:23
  22.2 33.9 %all-to-all-start = ((bf16[4,2,32768]{2,1,0:T(2,128)(2,1)}), bf16[4,2,32768]{2,1,0:T(2,128)(2,1)S(1)}, u32[]{:S(2)}, u32[]{:S(2)}) async-start(bf16[4,2,32768]{2,1,0:T(2,128)(2,1)} %reshape.27), calls=%async_computation | async-start | bytes 1048576 | tf_op jit(solution)/shard_map/all_to_all | solution.py:34
  142.9 50.3 %copy-start.2 = (f32[64,64]{1,0:T(8,128)}, f32[64,64]{1,0:T(8,128)S(1)}, u32[]{:S(2)}) copy-start(f32[64,64]{1,0:T(8,128)S(1)} %broadcast_divide_fusion) | copy-start | bytes 49156
  186.6 6.7 %copy-start.1 = (bf16[64,70,1024]{2,0,1:T(8,128)(2,1)S(1)}, bf16[64,70,1024]{2,0,1:T(8,128)(2,1)}, u32[]{:S(2)}) copy-start(bf16[64,70,1024]{2,0,1:T(8,128)(2,1)} %all-gather.2.cloned.1.call-done) | copy-start | bytes 27525124
Sparse Core Ops, SparseCore 0:
  9.6 176.9 all-gather.1
where the time goes:
time: 203 us
  waiting for transfers between devices  69.2 us (34%)
  blocking collectives  63.8 us (31%)
  local copies, waits for them, and re-layouts  22.2 us (11%)
  other arithmetic  19.3 us (10%)
  between operations  14.1 us (7%)
  matrix products  7.83 us (4%)
  starting transfers between devices  6.41 us (3%)
    psum x1, blocking collectives, per_device(): lax.psum((partial_gram, weight_sum), ('mem', 'space'))  63.8 us
    all_gather x1, waiting for transfers between devices, per_device(): members_block = lax.all_gather(ensemble, 'mem', axis=0, tiled=True)  42.6 us
    all_to_all x1, waiting for transfers between devices, per_device(): lax.all_to_all(observed.astype(jnp.bfloat16), 'mem', split_axis=2, concat...  25.9 us
    unnamed x9, local copies, waits for them, and re-layouts  10.8 us
    reduce_sum x1, other arithmetic, per_device(): totals = jnp.sum(members_block, axis=0, dtype=jnp.float32)  6.65 us
    convert_element_type x1, local copies, waits for them, and re-layouts, per_device(): by_columns = lax.all_to_all(observed.astype(jnp.bfloat16), 'mem', split_a...  6.59 us
    all_to_all x1, starting transfers between devices, per_device(): lax.all_to_all(observed.astype(jnp.bfloat16), 'mem', split_axis=2, concat...  6.38 us
    convert_element_type x1, other arithmetic, per_device(): by_columns = lax.all_to_all(observed.astype(jnp.bfloat16), 'mem', split_a...  6.11 us
  transfers between devices with their start and end apart: 2, of which 2 were waited for; matrix products, arithmetic and copies ran while one was open for 20% of the time, Pallas kernels for 0%

commit v1 on v0

--- a/solution.py
+++ b/solution.py
@@ -31,8 +31,14 @@
     member_mean = totals / MEMBERS
     analysis = (combined + member_mean[None, :, :] * keep_mean[:, None, None]).astype(jnp.bfloat16)
     observed = jnp.einsum("ov,mvc->moc", obs_operator, ensemble, preferred_element_type=jnp.float32)
-    by_columns = lax.all_to_all(
-        observed.astype(jnp.bfloat16), "mem", split_axis=2, concat_axis=0, tiled=True
+    by_columns = jnp.concatenate(
+        lax.all_to_all(
+            jnp.stack(jnp.split(observed.astype(jnp.bfloat16), lax.axis_size("mem"), axis=2)),
+            "mem",
+            0,
+            0,
+        ),
+        axis=0,
     ).astype(observed.dtype)
     cells_here = by_columns.shape[2]
     own_weights = lax.dynamic_slice_in_dim(

time: 203 us -> 198 us (0.975)
  local copies, waits for them, and re-layouts: 22.2 us -> 0.21 us
  waiting for transfers between devices: 69.2 us -> 89.9 us
  other arithmetic: 19.3 us -> 9.92 us
  blocking collectives: 63.8 us -> 68.2 us
    all_gather x1, waiting for transfers between devices: 42.6 us -> 66 us  [per_device(): members_block = lax.all_gather(ensemble, 'mem', axis=0, tiled=True)]
    convert_element_type x2 -> x0, local copies, waits for them, and re-layouts: 11.3 us -> none  [the longest x1 6.59 us: per_device(): by_columns = lax.all_to_all(observed.astype(jnp.bfloat16), 'mem', split_a...]
    unnamed x9 -> x7, local copies, waits for them, and re-layouts: 10.8 us -> 0.1 us
    convert_element_type x1, other arithmetic: 6.11 us -> 0.17 us  [per_device(): by_columns = jnp.concatenate(lax.all_to_all(jnp.stack(jnp.split(observed....]
    psum x1, blocking collectives: 63.8 us -> 68.2 us  [per_device(): lax.psum((partial_gram, weight_sum), ('mem', 'space'))]
    reduce_sum x2 -> x1, other arithmetic: 4.27 us -> 0.1 us  [gram_terms(): departures = observed - jnp.sum(observed, axis=0) / MEMBERS]
    all_to_all x1, waiting for transfers between devices: 25.9 us -> 23.1 us  [per_device(): lax.all_to_all(jnp.stack(jnp.split(observed.astype(jnp.bfloat16), lax.axi...]
  transfers between devices with their start and end apart: 2 -> 2, of which waited for: 2 -> 2; matrix products, arithmetic and copies ran while one was open for 20% -> 5% of each run, Pallas kernels for 0% -> 0%
where the time goes in v1:
time: 198 us
  waiting for transfers between devices  89.9 us (45%)
  blocking collectives  68.2 us (34%)
  between operations  14.1 us (7%)
  other arithmetic  9.92 us (5%)
  matrix products  8.91 us (4%)
  starting transfers between devices  6.38 us (3%)
    psum x1, blocking collectives, per_device(): lax.psum((partial_gram, weight_sum), ('mem', 'space'))  68.2 us
    all_gather x1, waiting for transfers between devices, per_device(): members_block = lax.all_gather(ensemble, 'mem', axis=0, tiled=True)  66 us
    all_to_all x1, waiting for transfers between devices, per_device(): lax.all_to_all(jnp.stack(jnp.split(observed.astype(jnp.bfloat16), lax.axi...  23.1 us
    reduce_sum x1, other arithmetic, per_device(): totals = jnp.sum(members_block, axis=0, dtype=jnp.float32)  6.65 us
    all_to_all x1, starting transfers between devices, per_device(): lax.all_to_all(jnp.stack(jnp.split(observed.astype(jnp.bfloat16), lax.axi...  6.35 us
  transfers between devices with their start and end apart: 2, of which 2 were waited for; matrix products, arithmetic and copies ran while one was open for 5% of the time, Pallas kernels for 0%

profile of v1, /device:TPU:0, one launch (start us, length us, event | category | flops | bytes accessed | tf_op | source)
XLA Modules:
  0.0 197.6 jit_solution(8026389074448474218)
XLA Ops:
  7.2 0.0 copy-start
  7.2 0.0 all-gather.2.cloned.1.call-start
  7.2 0.7 all-gather.2.cloned.1.call-update
  7.9 3.0 %fusion.7 = bf16[16,16,1024]{2,1,0:T(8,128)(2,1)S(1)} fusion(bf16[16,70,1024]{2,0,1:T(8,128)(2,1)} %param.4, bf16[16,70]{1,0:T(8,128)(2,1)} %param.6), kind=kOutput, calls=%fused_computation.7 | convolution fusion | flops 36962304 | bytes 2820288 | tf_op jit(solution)/shard_map/ov,mvc->moc/dot_general | solution.py:33
  10.9 0.9 pad_maximum_fusion
  11.8 6.3 %all-to-all-start = ((bf16[4,16,16,256]{3,2,1,0:T(8,128)(2,1)}), bf16[4,16,16,256]{3,2,1,0:T(8,128)(2,1)S(1)}, u32[]{:S(2)}, u32[]{:S(2)}) async-start(bf16[4,16,16,256]{3,2,1,0:T(8,128)(2,1)} %pad_maximum_fusion), calls=%async_computation | async-start | bytes 1048576 | tf_op jit(solution)/shard_map/all_to_all | solution.py:35
  18.2 0.0 copy-done
  18.2 0.1 constant_dynamic-slice_fusion.1
  18.2 0.1 copy.10
  18.3 0.1 convert_reduce_fusion.2
  18.4 1.3 fusion.17
  19.8 23.1 %all-to-all-done = bf16[4,16,16,256]{3,2,1,0:T(8,128)(2,1)S(1)} async-done(((bf16[4,16,16,256]{3,2,1,0:T(8,128)(2,1)}), bf16[4,16,16,256]{3,2,1,0:T(8,128)(2,1)S(1)}, u32[]{:S(2)}, u32[]{:S(2)}) %all-to-all-start) | async-done | bytes 524320 | tf_op jit(solution)/shard_map/all_to_all | solution.py:35
  42.9 0.1 convert_reduce_fusion.1
  43.0 0.2 bitcast_convert_fusion
  43.2 2.1 %fusion.10 = f32[64,64]{1,0:T(8,128)S(1)} fusion(f32[64,16,256]{2,1,0:T(8,128)S(1)} %bitcast_convert_fusion, f32[16,256]{1,0:T(8,128)S(1)} %get-tuple-element.6, f32[16,256]{1,0:T(8,128)S(1)} %broadcast_multiply_fusion.1), kind=kOutput, calls=%fused_computation.8 | convolution fusion | flops 202113024 | bytes 1097728 | tf_op jit(solution)/shard_map/ioc,joc->ij/dot_general | solution.py:13
  45.3 68.2 %all-reduce = (f32[64,64]{1,0:T(8,128)S(1)}, f32[]{:T(128)}) all-reduce(f32[64,64]{1,0:T(8,128)S(1)} %fusion.10, f32[]{:T(128)} %get-tuple-element.5), channel_id=1, replica_groups=mesh['parts'=2,'mem'=4,'space'=4] {'mem','space'}, use_global_device_ids=true, to_apply=%region_3.0 | all-reduce | flops 4097 | bytes 32776 | tf_op jit(solution)/shard_map/psum | solution.py:48
  113.5 0.7 broadcast_divide_fusion
  114.2 0.0 copy-start.2
  114.2 0.2 fusion.18
  114.4 0.8 fusion.19
  115.3 66.0 %all-gather.2.cloned.1.call-done = bf16[64,70,1024]{2,0,1:T(8,128)(2,1)} async-done(((bf16[16,70,1024]{2,0,1:T(8,128)(2,1)}), bf16[64,70,1024]{2,0,1:T(8,128)(2,1)}) %all-gather.2.cloned.1.call-update) | async-done | bytes 9175056 | tf_op jit(solution)/shard_map/all_gather | solution.py:23
  181.3 0.0 copy-start.1
  181.3 6.7 %convert_reduce_fusion = f32[70,1024]{1,0:T(8,128)S(1)} fusion(bf16[64,70,1024]{2,0,1:T(8,128)(2,1)} %all-gather.2.cloned.1.call-done), kind=kLoop, calls=%fused_computation | loop fusion | flops 9103360 | bytes 9461760 | tf_op jit(solution)/shard_map/reduce_sum | solution.py:27
  187.9 0.0 copy-done.2
  188.0 0.0 copy-done.1
  188.0 2.8 %add_convert_fusion = bf16[16,70,1024]{2,0,1:T(8,128)(2,1)} fusion(f32[16]{0:T(128)S(1)} %broadcast_subtract_fusion, f32[70,1024]{1,0:T(8,128)S(1)} %broadcast_multiply_fusion, bf16[64,70,1024]{2,0,1:T(8,128)(2,1)S(1)} %copy-done.1, bf16[64,16]{1,0:T(8,128)(2,1)S(1)} %constant_dynamic-slice_fusion.1), kind=kOutput, calls=%fused_computation.1 | convolution fusion | flops 150241280 | bytes 11757632 | tf_op jit(solution)/shard_map/kj,kvc->jvc/dot_general | solution.py:24
  (4 shorter events, 0.1 us)
Async XLA Ops:
  7.2 11.0 %copy-start = (bf16[64,64]{1,0:T(8,128)(2,1)S(1)}, bf16[64,64]{1,0:T(8,128)(2,1)}, u32[]{:S(2)}) copy-start(bf16[64,64]{1,0:T(8,128)(2,1)} %param.5) | copy-start | bytes 24580
  7.2 174.1 %all-gather.2.cloned.1.call-start = ((), (), s32[]{:S(2)}) async-start(), calls=%async_computation.1 | async-start | bytes 11468800 | tf_op jit(solution)/shard_map/all_gather | solution.py:23
  11.8 31.1 %all-to-all-start = ((bf16[4,16,16,256]{3,2,1,0:T(8,128)(2,1)}), bf16[4,16,16,256]{3,2,1,0:T(8,128)(2,1)S(1)}, u32[]{:S(2)}, u32[]{:S(2)}) async-start(bf16[4,16,16,256]{3,2,1,0:T(8,128)(2,1)} %pad_maximum_fusion), calls=%async_computation | async-start | bytes 1048576 | tf_op jit(solution)/shard_map/all_to_all | solution.py:35
  114.2 73.8 %copy-start.2 = (f32[64,64]{1,0:T(8,128)}, f32[64,64]{1,0:T(8,128)S(1)}, u32[]{:S(2)}) copy-start(f32[64,64]{1,0:T(8,128)S(1)} %broadcast_divide_fusion) | copy-start | bytes 49156
  181.3 6.7 %copy-start.1 = (bf16[64,70,1024]{2,0,1:T(8,128)(2,1)S(1)}, bf16[64,70,1024]{2,0,1:T(8,128)(2,1)}, u32[]{:S(2)}) copy-start(bf16[64,70,1024]{2,0,1:T(8,128)(2,1)} %all-gather.2.cloned.1.call-done) | copy-start | bytes 27525124
Sparse Core Ops, SparseCore 0:
  9.6 171.6 all-gather.1
